TPU v7x, 32 devices: a whole 2x2x4 slice. The times are simulated.
32 devices in a mesh: batch: 8 (over z, y), cols: 2 (over core), ens: 2 (over x).
Axes of the slice: x: 2, y: 2, z: 4, core: 2. Of those that a mesh axis runs over, the one named last changes fastest.
Arguments:
- slope_up: float32 [16, 1280, 5120], P(('ens', 'batch'), None, 'cols'), parts along dimension 0, may hold values from -0.875 to 0.875
- slope_down: float32 [16, 5120, 1280], P(('ens', 'batch'), 'cols'), parts along dimension 0, may hold values from -0.875 to 0.875
- slope_norm: float32 [16, 1280], P(('ens', 'batch')), parts along dimension 0, may hold values from -8 to 8
- slope_bias: float32 [16, 1280], P(('ens', 'batch')), parts along dimension 0, may hold values from -8 to 8
- param_up: float32 [2560, 5120], P(('ens', 'batch'), 'cols'), parts along dimension 0, may hold values from -0.25 to 0.25
- param_down: float32 [10240, 1280], P(('ens', 'cols'), 'batch'), parts along dimension 0, may hold values from -0.125 to 0.125
- param_norm: float32 [2560], P(('ens', 'batch')), parts along dimension 0, may hold values from 0.25 to 1.75
- param_bias: float32 [2560], P(('ens', 'batch')), parts along dimension 0, may hold values from -3 to 3
Outputs:
- half_up: bfloat16 [2560, 5120], P('ens', 'cols'), parts along dimension 0
- half_down: bfloat16 [10240, 1280], P(('ens', 'cols')), parts along dimension 0
- half_norm: bfloat16 [2560], P('ens'), parts along dimension 0
- half_bias: bfloat16 [2560], P('ens'), parts along dimension 0
- next_up: float32 [2560, 5120], P(('ens', 'batch'), 'cols'), parts along dimension 0
- next_down: float32 [10240, 1280], P(('ens', 'cols'), 'batch'), parts along dimension 0
- next_norm: float32 [2560], P(('ens', 'batch')), parts along dimension 0
- next_bias: float32 [2560], P(('ens', 'batch')), parts along dimension 0
There are 2 independent parts, one for each index of `ens`. A program takes and returns all parts, laid end to end along the dimension named above; each array names one. Nothing has to cross between parts.
All inputs are finite; a program needn't handle non-finite values.
Results may differ from a plain program's by a relative error of at most 0.008.
Values may be sent and summed in bfloat16 or wider, within the bound.
A program may use at most 128 MiB of HBM per device.

v0:
```python
import jax
import jax.numpy as jnp
from jax import lax
from jax.sharding import PartitionSpec as P

learn_rate = 0.4


def on_device(
    slope_up, slope_down, slope_norm, slope_bias, param_up, param_down, param_norm, param_bias
):
    mean_up, mean_down = (
        lax.psum_scatter(
            slope_up[0].astype(jnp.bfloat16), "batch", scatter_dimension=0, tiled=True
        ).astype(jnp.float32),
        lax.psum_scatter(
            slope_down[0].astype(jnp.bfloat16), "batch", scatter_dimension=1, tiled=True
        ).astype(jnp.float32),
    )
    whole_norm, whole_bias = lax.psum((slope_norm[0], slope_bias[0]), "batch")
    place = lax.axis_index("batch")
    mean_norm = lax.dynamic_slice_in_dim(
        whole_norm, place * param_norm.shape[0], param_norm.shape[0]
    )
    mean_bias = lax.dynamic_slice_in_dim(
        whole_bias, place * param_bias.shape[0], param_bias.shape[0]
    )
    mean_rate = lax.axis_size("batch") ** (-0.5)
    mean_up = mean_up * mean_rate
    mean_down = mean_down * mean_rate
    mean_norm = mean_norm * mean_rate
    mean_bias = mean_bias * mean_rate
    own_up, own_down, slope_up_norm, slope_down_norm = lax.psum(
        (
            jnp.sum(param_up * param_up, axis=1, keepdims=True),
            jnp.sum(param_down * param_down, axis=0, keepdims=True),
            jnp.sum(mean_up * mean_up, axis=1, keepdims=True),
            jnp.sum(mean_down * mean_down, axis=0, keepdims=True),
        ),
        "cols",
    )
    mean_up = mean_up * (jnp.sqrt(own_up) * lax.rsqrt(slope_up_norm + 1e-06))
    mean_down = mean_down * (jnp.sqrt(own_down) * lax.rsqrt(slope_down_norm + 1e-06))
    next_up = param_up - learn_rate * mean_up
    next_down = param_down - learn_rate * mean_down
    next_norm = param_norm - learn_rate * mean_norm
    next_bias = param_bias - learn_rate * mean_bias
    half_up, half_down, half_norm, half_bias = (
        lax.all_gather(next_up.astype(jnp.bfloat16), "batch", axis=0, tiled=True),
        lax.all_gather(next_down.astype(jnp.bfloat16), "batch", axis=1, tiled=True),
        lax.all_gather(next_norm.astype(jnp.bfloat16), "batch", axis=0, tiled=True),
        lax.all_gather(next_bias.astype(jnp.bfloat16), "batch", axis=0, tiled=True),
    )
    return (half_up, half_down, half_norm, half_bias, next_up, next_down, next_norm, next_bias)


def solution(mesh):
    return jax.shard_map(
        on_device,
        mesh=mesh,
        in_specs=(
            P(("ens", "batch"), None, "cols"),
            P(("ens", "batch"), "cols", None),
            P(("ens", "batch"), None),
            P(("ens", "batch"), None),
            P(("ens", "batch"), "cols"),
            P(("ens", "cols"), "batch"),
            P(("ens", "batch")),
            P(("ens", "batch")),
        ),
        out_specs=(
            P("ens", "cols"),
            P(("ens", "cols"), None),
            P("ens"),
            P("ens"),
            P(("ens", "batch"), "cols"),
            P(("ens", "cols"), "batch"),
            P(("ens", "batch")),
            P(("ens", "batch")),
        ),
        check_vma=False,
    )
```

profile of v0, /device:TPU:0, one launch (start us, length us, event | category | flops | bytes accessed | tf_op | source)
XLA Modules:
  0.0 499.8 jit_solution(5791196715308530300)
XLA Ops:
  7.2 8.3 %convert_bitcast_fusion.1 = bf16[1280,2560]{1,0:T(8,128)(2,1)} fusion(f32[1,1280,2560]{2,1,0:T(8,128)} %param.8), kind=kLoop, calls=%fused_computation.1 | loop fusion | flops 3276800 | bytes 19660800 | tf_op jit(solution)/shard_map/convert_element_type | solution.py:14
  15.6 11.2 %copy.18 = bf16[1,2560,1280]{1,2,0:T(8,128)(2,1)} copy(f32[1,2560,1280]{2,1,0:T(8,128)} %param.9) | data formatting | bytes 19660800 | tf_op args[1]
  26.9 0.0 all-gather.3.cloned.1.call-start
  26.9 1.3 copy-done
  28.2 0.2 multiply_reduce_fusion.1
  28.4 0.3 copy-done.1
  28.7 0.2 multiply_reduce_fusion
  28.9 111.3 %reduce-scatter.3.cloned.1.call-done = bf16[160,2560]{1,0:T(8,128)(2,1)} async-done(((bf16[1280,2560]{1,0:T(8,128)(2,1)}), bf16[160,2560]{1,0:T(8,128)(2,1)}) %reduce-scatter.3.cloned.1.call-update) | async-done | bytes 819216 | tf_op jit(solution)/shard_map/reduce_scatter | solution.py:13
  140.2 1.4 fusion.1
  141.7 123.7 %reduce-scatter.5.cloned.1.call-done = bf16[2560,160]{0,1:T(8,128)(2,1)} async-done(((bf16[2560,1280]{0,1:T(8,128)(2,1)}), bf16[2560,160]{0,1:T(8,128)(2,1)}) %reduce-scatter.5.cloned.1.call-update) | async-done | bytes 819216 | tf_op jit(solution)/shard_map/reduce_scatter | solution.py:16
  265.4 1.4 fusion.5
  266.8 2.5 all-reduce.3
  269.3 2.9 fusion.12
  272.4 2.9 fusion.10
  275.5 0.6 dynamic-slice
  276.7 37.1 %all-reduce.2 = (f32[1280]{0:T(1024)S(1)}, f32[1280]{0:T(1024)S(1)}) all-reduce(f32[1280]{0:T(1024)S(1)} %reduce, f32[1280]{0:T(1024)S(1)} %reduce.1), channel_id=1, replica_groups=mesh['batch'=8,'cols'=2,'ens'=2] {'batch'}, use_global_device_ids=true, to_apply=%region_10.0 | all-reduce | flops 2560 | bytes 20480 | tf_op jit(solution)/shard_map/psum | solution.py:20
  313.8 0.6 fusion.8
  314.5 0.2 dynamic-update-slice
  314.7 0.2 dynamic-update-slice.1
  314.9 19.5 %all-reduce.4 = (bf16[1280]{0:T(1024)(128)(2,1)}, bf16[1280]{0:T(1024)(128)(2,1)}) all-reduce(bf16[1280]{0:T(1024)(128)(2,1)S(1)} %dynamic-update-slice, bf16[1280]{0:T(1024)(128)(2,1)S(1)} %dynamic-update-slice.1), channel_id=1, replica_groups=mesh['batch'=8,'cols'=2,'ens'=2] {'batch'}, use_global_device_ids=true, to_apply=%add | all-reduce | flops 2560 | bytes 10240
  334.4 40.3 %all-gather.3.cloned.1.call-done = bf16[1280,2560]{1,0:T(8,128)(2,1)} async-done(((bf16[160,2560]{1,0:T(8,128)(2,1)}), bf16[1280,2560]{1,0:T(8,128)(2,1)}) %all-gather.3.cloned.1.call-update) | async-done | bytes 6553616 | tf_op jit(solution)/shard_map/all_gather | solution.py:49
  374.7 103.0 %all-gather.5.cloned.1.call-done = bf16[2560,1280]{0,1:T(8,128)(2,1)} async-done(((bf16[2560,160]{0,1:T(8,128)(2,1)}), bf16[2560,1280]{0,1:T(8,128)(2,1)}) %all-gather.5.cloned.1.call-update) | async-done | bytes 6553616 | tf_op jit(solution)/shard_map/all_gather | solution.py:50
  477.7 9.5 %copy.19 = bf16[2560,1280]{1,0:T(8,128)(2,1)} copy(bf16[2560,1280]{0,1:T(8,128)(2,1)} %all-gather.5.cloned.1.call-done) | data formatting | bytes 13107200
  487.2 6.1 %copy.23 = bf16[1280,2560]{1,0:T(8,128)(2,1)} copy(bf16[1280,2560]{1,0:T(8,128)(2,1)} %all-gather.3.cloned.1.call-done) | data formatting | bytes 13107200
  (25 shorter events, 0.3 us)
Async XLA Ops:
  7.2 133.0 %reduce-scatter.3.cloned.1.call-start = ((), (), s32[]{:S(2)}) async-start(), calls=%async_computation.2 | async-start | bytes 7372800 | tf_op jit(solution)/shard_map/reduce_scatter | solution.py:13
  15.5 249.9 %reduce-scatter.5.cloned.1.call-start = ((), (), s32[]{:S(2)}) async-start(), calls=%async_computation.4 | async-start | bytes 7372800 | tf_op jit(solution)/shard_map/reduce_scatter | solution.py:16
  26.8 1.4 copy-start
  26.8 1.9 copy-start.1
  26.9 347.9 %all-gather.3.cloned.1.call-start = ((), (), s32[]{:S(2)}) async-start(), calls=%async_computation.3 | async-start | bytes 7372800 | tf_op jit(solution)/shard_map/all_gather | solution.py:49
  272.3 205.4 %all-gather.5.cloned.1.call-start = ((), (), s32[]{:S(2)}) async-start(), calls=%async_computation.5 | async-start | bytes 7372800 | tf_op jit(solution)/shard_map/all_gather | solution.py:50
  272.3 3.0 copy-start.2
  272.4 3.1 copy-start.3
  272.4 3.1 copy-start.6
  272.4 41.5 %copy-start.4 = (f32[160]{0:T(256)S(1)}, f32[160]{0:T(256)}, u32[]{:S(2)}) copy-start(f32[160]{0:T(256)} %param.15) | copy-start | bytes 1924
  272.4 41.5 %copy-start.5 = (f32[160]{0:T(256)S(1)}, f32[160]{0:T(256)}, u32[]{:S(2)}) copy-start(f32[160]{0:T(256)} %param.14) | copy-start | bytes 1924
Sparse Core Ops, SparseCore 0:
  15.7 124.5 reduce-scatter.2
  144.4 120.9 reduce-scatter.4
  272.4 102.2 all-gather.2
  377.3 100.3 all-gather.4
where the time goes:
time: 501 us; the launch traced here: 500 us
  waiting for transfers between devices  378 us (75%)
  blocking collectives  59.1 us (12%)
  local copies, waits for them, and re-layouts  29.5 us (6%)
  other arithmetic  18.2 us (4%)
  between operations  14.5 us (3%)
    reduce_scatter x1, waiting for transfers between devices, on_device(): lax.psum_scatter(slope_down[0].astype(jnp.bfloat16), 'batch', scatter_dim...  124 us
    reduce_scatter x1, waiting for transfers between devices, on_device(): lax.psum_scatter(slope_up[0].astype(jnp.bfloat16), 'batch', scatter_dimen...  111 us
    all_gather x1, waiting for transfers between devices, on_device(): lax.all_gather(next_down.astype(jnp.bfloat16), 'batch', axis=1, tiled=True)  103 us
    all_gather x1, waiting for transfers between devices, on_device(): lax.all_gather(next_up.astype(jnp.bfloat16), 'batch', axis=0, tiled=True)  40.3 us
    psum x1, blocking collectives, on_device(): whole_norm, whole_bias = lax.psum((slope_norm[0], slope_bias[0]), 'batch')  37.1 us
    unnamed x22, local copies, waits for them, and re-layouts  29.5 us
    unnamed x1, blocking collectives  19.5 us
  transfers between devices with their start and end apart: 4, of which 4 were waited for; matrix products, arithmetic and copies ran while one was open for 4% of the time, Pallas kernels for 0%

commit v1 on v0

v1 whole, which is shorter than its diff:
```python
import functools

import jax
import jax.numpy as jnp
from jax import lax
from jax.experimental import pallas as pl
from jax.experimental.pallas import tpu as pltpu
from jax.sharding import PartitionSpec as P

learn_rate = 0.4
MESH = pl.DeviceIdType.MESH
R = 16
LANE = 128
F32, BF16 = jnp.float32, jnp.bfloat16


def kernel(
    n,
    m,
    LA,
    up_ref,
    down_ref,
    pup_ref,
    pdown_ref,
    vec_ref,
    half_ref,
    next_ref,
    sums_ref,
    stage,
    XA,
    XB,
    RYA,
    RYB,
    RZA,
    RZB,
    NX,
    PR,
    SQ,
    GA,
    GB,
    VG,
    up_sem,
    down_sem,
    par_sem,
    out_sem,
    send,
    recv,
    sq_send,
    sq_recv,
    v_send,
    v_recv,
):
    Z = n // 2
    C = NX.shape[0]
    CH = C // 2
    L = NX.shape[2]
    me = lax.axis_index("batch")
    core = lax.axis_index("cols")
    z = me // 2
    y = me % 2
    other = z * 2 + 1 - y
    rate = n ** (-0.5)

    def load_up(c):
        return pltpu.make_async_copy(up_ref.at[:, :, c], stage.at[c % 2], up_sem.at[c % 2])

    def load_down(c):
        k = c - CH
        return [
            pltpu.make_async_copy(
                down_ref.at[:, 0, k, :, pl.ds(0, LA)], XA.at[c, 0], down_sem.at[0, k]
            ),
            pltpu.make_async_copy(
                down_ref.at[:, 1, k, :, pl.ds(0, LA)], XA.at[c, 1], down_sem.at[1, k]
            ),
            pltpu.make_async_copy(
                down_ref.at[:, :, k, :, pl.ds(LA, L - LA)], XB.at[c], down_sem.at[2, k]
            ),
        ]

    def load_params():
        return [
            pltpu.make_async_copy(pup_ref, PR.at[pl.ds(0, CH)], par_sem.at[0]),
            pltpu.make_async_copy(pdown_ref, PR.at[pl.ds(CH, CH)], par_sem.at[1]),
        ]

    load_up(0).start()
    for d in load_params():
        d.start()

    @pl.loop(CH, C)
    def _(c):
        for d in load_down(c):
            d.start()

    barrier = pltpu.get_barrier_semaphore()
    for o in range(1, n):
        pl.semaphore_signal(
            barrier, inc=1, device_id={"batch": (me + o) % n}, device_id_type=MESH
        )
    for o in range(1, m):
        pl.semaphore_signal(
            barrier, inc=1, device_id={"cols": (core + o) % m}, device_id_type=MESH
        )
    pl.semaphore_wait(barrier, n - 1 + m - 1)

    def remote(src, dst, kind, c, to):
        return pltpu.make_async_remote_copy(
            src_ref=src,
            dst_ref=dst,
            send_sem=send.at[kind, c],
            recv_sem=recv.at[kind, c],
            device_id={"batch": to},
            device_id_type=MESH,
        )

    def vec_copy(o):
        return pltpu.make_async_remote_copy(
            src_ref=vec_ref,
            dst_ref=VG.at[o - 1],
            send_sem=v_send.at[o - 1],
            recv_sem=v_recv.at[o - 1],
            device_id={"batch": (me + o) % n},
            device_id_type=MESH,
        )

    for o in range(1, n):
        vec_copy(o).start()

    def sq_copy(c, o):
        return pltpu.make_async_remote_copy(
            src_ref=SQ.at[c, 0],
            dst_ref=SQ.at[c, o],
            send_sem=sq_send.at[o - 1, c],
            recv_sem=sq_recv.at[o - 1, c],
            device_id={"cols": (core + o) % m},
            device_id_type=MESH,
        )

    YA, YB, RA, LFA, RB, LFB, GYA, GYB, GRA, GLA, GRB, GLB = range(12)

    def ya(c):
        return remote(XA.at[c, 1 - y], RYA.at[c], YA, c, other)

    def yb(c):
        return remote(XB.at[c, z, 1 - y], RYB.at[c], YB, c, other)

    def gya(c):
        return remote(GA.at[c, y], GA.at[c, y], GYA, c, other)

    def gya_in(c):
        return remote(GA.at[c, 1 - y], GA.at[c, 1 - y], GYA, c, other)

    def gyb(c):
        return remote(GB.at[c, z, y], GB.at[c, z, y], GYB, c, other)

    def gyb_in(c):
        return remote(GB.at[c, z, 1 - y], GB.at[c, z, 1 - y], GYB, c, other)

    def x_ref(first, c):
        return XA.at[c, y] if first else XB.at[c]

    def sum_right(first, c, k):
        rz = RZA if first else RZB
        return remote(
            x_ref(first, c).at[pl.ds(k + 1, Z - 1 - k)],
            rz.at[c, pl.ds(k + 2, Z - 1 - k)],
            RA if first else RB,
            c,
            jnp.minimum(me + 2, n - 1),
        )

    def sum_left(first, c, k):
        rz = RZA if first else RZB
        return remote(
            x_ref(first, c).at[pl.ds(0, k)],
            rz.at[c, pl.ds(0, k)],
            LFA if first else LFB,
            c,
            jnp.maximum(me - 2, 0),
        )

    def add(first, c, lo, count, slot):
        rz = RZA if first else RZB
        for d in range(count):
            if first:
                XA[c, y, lo + d] = (
                    XA[c, y, lo + d].astype(F32) + rz[c, slot + d].astype(F32)
                ).astype(BF16)
            else:
                XB[c, lo + d] = (
                    XB[c, lo + d].astype(F32) + rz[c, slot + d].astype(F32)
                ).astype(BF16)

    def reduce_step(first, t):
        for k in range(Z):

            @pl.when((z == k) & (t - k >= 0) & (t - k < C))
            def _():
                c = t - k
                if k > 0:
                    sum_right(first, c, k - 1).wait_recv()
                    add(first, c, k, Z - k, k + 1)
                if k < Z - 1:
                    sum_right(first, c, k).start()

            q = Z - 1 - k

            @pl.when((z == k) & (t - q >= 0) & (t - q < C))
            def _():
                c = t - q
                if k < Z - 1:
                    sum_left(first, c, k + 1).wait_recv()
                    add(first, c, 0, k + 1, 0)
                if k > 0:
                    sum_left(first, c, k).start()

    def g_ref(first, c):
        return GA.at[c, y] if first else GB.at[c]

    def gather_right(first, c, k):
        ref = g_ref(first, c).at[pl.ds(0, k + 1)]
        return remote(ref, ref, GRA if first else GRB, c, jnp.minimum(me + 2, n - 1))

    def gather_left(first, c, k):
        ref = g_ref(first, c).at[pl.ds(k, Z - k)]
        return remote(ref, ref, GLA if first else GLB, c, jnp.maximum(me - 2, 0))

    def gather_step(first, t):
        for k in range(Z):

            @pl.when((z == k) & (t - k >= 0) & (t - k < C))
            def _():
                c = t - k
                if k > 0:
                    gather_right(first, c, k - 1).wait_recv()
                if k < Z - 1:
                    gather_right(first, c, k).start()

            q = Z - 1 - k

            @pl.when((z == k) & (t - q >= 0) & (t - q < C))
            def _():
                c = t - q
                if k < Z - 1:
                    gather_left(first, c, k + 1).wait_recv()
                if k > 0:
                    gather_left(first, c, k).start()

    def outs(c):
        w = c // CH
        k = c % CH
        return [
            pltpu.make_async_copy(
                GA.at[c, 0], half_ref.at[w, :, 0, k, :, pl.ds(0, LA)], out_sem.at[0, c]
            ),
            pltpu.make_async_copy(
                GA.at[c, 1], half_ref.at[w, :, 1, k, :, pl.ds(0, LA)], out_sem.at[1, c]
            ),
            pltpu.make_async_copy(
                GB.at[c], half_ref.at[w, :, :, k, :, pl.ds(LA, L - LA)], out_sem.at[2, c]
            ),
        ]

    def next_out(c):
        return pltpu.make_async_copy(NX.at[c], next_ref.at[c], out_sem.at[3, c])

    def lanes(x):
        s = x[:, :LANE] * x[:, :LANE]
        for i in range(1, L // LANE):
            part = x[:, i * LANE : (i + 1) * LANE]
            s = s + part * part
        return s

    def when_chunk(c):
        return pl.when((c >= 0) & (c < C))

    @pl.loop(0, C + 2 * Z + 2)
    def _(t):
        @pl.when(t + 1 < CH)
        def _():
            load_up(t + 1).start()

        @pl.when(t < CH)
        def _():
            load_up(t).wait()
            for d in range(Z):
                for v in range(2):
                    XA[t, v, d] = stage[t % 2, d, v, :, :LA].astype(BF16)
                    XB[t, d, v] = stage[t % 2, d, v, :, LA:].astype(BF16)

        @pl.when((t >= CH) & (t < C))
        def _():
            for d in load_down(t):
                d.wait()

        @pl.when(t < C)
        def _():
            ya(t).start()

        reduce_step(False, t)
        s = t - 1

        @when_chunk(s)
        def _():
            ya(s).wait_recv()
            for d in range(Z):
                XA[s, y, d] = (XA[s, y, d].astype(F32) + RYA[s, d].astype(F32)).astype(BF16)

        reduce_step(True, s)
        b = t - (Z - 1)

        @when_chunk(b)
        def _():
            yb(b).start()

        f = t - Z

        @pl.when(f == 0)
        def _():
            for d in load_params():
                d.wait()

        @when_chunk(f)
        def _():
            yb(f).wait_recv()
            NX[f, :, :LA] = XA[f, y, z].astype(F32) * rate
            NX[f, :, LA:] = (XB[f, z, y].astype(F32) + RYB[f].astype(F32)) * rate
            SQ[f, 0, 0] = lanes(NX[f])
            SQ[f, 0, 1] = lanes(PR[f])
            for o in range(1, m):
                sq_copy(f, o).start()

        u = t - Z - 1

        @when_chunk(u)
        def _():
            for o in range(1, m):
                sq_copy(u, o).wait_recv()
            g = SQ[u, 0, 0]
            p = SQ[u, 0, 1]
            for o in range(1, m):
                g = g + SQ[u, o, 0]
                p = p + SQ[u, o, 1]
            g = jnp.sum(g, axis=1, keepdims=True)
            p = jnp.sum(p, axis=1, keepdims=True)
            scale = learn_rate * (jnp.sqrt(p) * lax.rsqrt(g + 1e-06))
            new = PR[u] - NX[u] * scale
            NX[u] = new
            half = new.astype(BF16)
            GA[u, y, z] = half[:, :LA]
            GB[u, z, y] = half[:, LA:]
            gyb(u).start()
            next_out(u).start()

        gather_step(True, u)

        @when_chunk(u - 1)
        def _():
            gyb_in(u - 1).wait_recv()

        gather_step(False, u - 1)

        @when_chunk(u - (Z - 1))
        def _():
            gya(u - (Z - 1)).start()

        e = u - Z

        @when_chunk(e)
        def _():
            gya_in(e).wait_recv()
            for d in outs(e):
                d.start()

    total = vec_ref[...]
    for o in range(1, n):
        vec_copy(o).wait()
        total = total + VG[o - 1]
    sums_ref[...] = total

    @pl.loop(0, C)
    def _(c):
        for d in outs(c):
            d.wait()
        next_out(c).wait()
        for d in (ya(c), yb(c), gya(c), gyb(c)):
            d.wait_send()
        for o in range(1, m):
            sq_copy(c, o).wait_send()
        for k in range(Z):

            @pl.when(z == k)
            def _():
                for first in (True, False):
                    if k < Z - 1:
                        sum_right(first, c, k).wait_send()
                        gather_right(first, c, k).wait_send()
                    if k > 0:
                        sum_left(first, c, k).wait_send()
                        gather_left(first, c, k).wait_send()


def on_device(
    slope_up, slope_down, slope_norm, slope_bias, param_up, param_down, param_norm, param_bias
):
    n = lax.axis_size("batch")
    m = lax.axis_size("cols")
    Z = n // 2
    rows, L = param_up.shape
    CH = rows // R
    C = 2 * CH
    LA = max(1, round(0.6 * L / LANE)) * LANE
    LB = L - LA
    width = slope_norm.shape[1]
    place = lax.axis_index("batch")
    up = slope_up[0].reshape(Z, 2, CH, R, L)
    down = slope_down[0].astype(BF16).T.reshape(Z, 2, CH, R, L)
    pup = param_up.reshape(CH, R, L)
    pdown = param_down.T.reshape(CH, R, L)
    mine = lax.dynamic_update_slice(
        jnp.zeros((2, width), F32), jnp.stack([param_norm, param_bias]), (0, place * rows)
    )
    vec = jnp.concatenate([slope_norm, slope_bias, mine], axis=0).reshape(8, width // 2)
    kinds = 12
    hbm = pl.BlockSpec(memory_space=pl.ANY)
    vmem = pl.BlockSpec(memory_space=pltpu.VMEM)
    half, new, sums = pl.pallas_call(
        functools.partial(kernel, n, m, LA),
        out_shape=(
            jax.ShapeDtypeStruct((2, Z, 2, CH, R, L), BF16),
            jax.ShapeDtypeStruct((C, R, L), F32),
            jax.ShapeDtypeStruct(vec.shape, F32),
        ),
        in_specs=[hbm, hbm, hbm, hbm, vmem],
        out_specs=(hbm, hbm, vmem),
        scratch_shapes=[
            pltpu.VMEM((2, Z, 2, R, L), F32),
            pltpu.VMEM((C, 2, Z, R, LA), BF16),
            pltpu.VMEM((C, Z, 2, R, LB), BF16),
            pltpu.VMEM((C, Z, R, LA), BF16),
            pltpu.VMEM((C, R, LB), BF16),
            pltpu.VMEM((C, Z + 1, R, LA), BF16),
            pltpu.VMEM((C, Z + 1, 2, R, LB), BF16),
            pltpu.VMEM((C, R, L), F32),
            pltpu.VMEM((C, R, L), F32),
            pltpu.VMEM((C, m, 2, R, LANE), F32),
            pltpu.VMEM((C, 2, Z, R, LA), BF16),
            pltpu.VMEM((C, Z, 2, R, LB), BF16),
            pltpu.VMEM((n - 1,) + vec.shape, F32),
            pltpu.SemaphoreType.DMA((2,)),
            pltpu.SemaphoreType.DMA((3, CH)),
            pltpu.SemaphoreType.DMA((2,)),
            pltpu.SemaphoreType.DMA((4, C)),
            pltpu.SemaphoreType.DMA((kinds, C)),
            pltpu.SemaphoreType.DMA((kinds, C)),
            pltpu.SemaphoreType.DMA((m - 1, C)),
            pltpu.SemaphoreType.DMA((m - 1, C)),
            pltpu.SemaphoreType.DMA((n - 1,)),
            pltpu.SemaphoreType.DMA((n - 1,)),
        ],
        compiler_params=pltpu.CompilerParams(
            collective_id=0, has_side_effects=True, vmem_limit_bytes=67043328
        ),
    )(up, down, pup, pdown, vec)
    half_up = half[0].reshape(n * rows, L)
    half_down = half[1].reshape(n * rows, L).T
    next_up = new[:CH].reshape(rows, L)
    next_down = new[CH:].reshape(rows, L).T
    sums = sums.reshape(4, width)
    whole = sums[2:] - learn_rate * (sums[:2] * n ** (-0.5))
    own = lax.dynamic_slice_in_dim(whole, place * rows, rows, axis=1)
    halves = whole.astype(BF16)
    return (half_up, half_down, halves[0], halves[1], next_up, next_down, own[0], own[1])


def solution(mesh):
    return jax.shard_map(
        on_device,
        mesh=mesh,
        in_specs=(
            P(("ens", "batch"), None, "cols"),
            P(("ens", "batch"), "cols", None),
            P(("ens", "batch"), None),
            P(("ens", "batch"), None),
            P(("ens", "batch"), "cols"),
            P(("ens", "cols"), "batch"),
            P(("ens", "batch")),
            P(("ens", "batch")),
        ),
        out_specs=(
            P("ens", "cols"),
            P(("ens", "cols"), None),
            P("ens"),
            P("ens"),
            P(("ens", "batch"), "cols"),
            P(("ens", "cols"), "batch"),
            P(("ens", "batch")),
            P(("ens", "batch")),
        ),
        check_vma=False,
    )
```

time: 501 us -> 304 us (0.61)
  waiting for transfers between devices: 378 us -> 0 us
  Pallas kernels: 0 us -> 260 us
  blocking collectives: 59.1 us -> 0 us
  between operations: 14.5 us -> 0.67 us
  other arithmetic: 18.2 us -> 10.4 us
    pallas_call x0 -> x1, Pallas kernels: none -> 260 us  [on_device(): pl.pallas_call(functools.partial(kernel, n, m, LA), out_shape=(jax.ShapeD...]
    reduce_scatter x2 -> x0, waiting for transfers between devices: 235 us -> none  [the longest x1 124 us: on_device(): lax.psum_scatter(slope_down[0].astype(jnp.bfloat16), 'batch', scatter_dim...]
    all_gather x2 -> x0, waiting for transfers between devices: 143 us -> none  [the longest x1 103 us: on_device(): lax.all_gather(next_down.astype(jnp.bfloat16), 'batch', axis=1, tiled=True)]
    psum x2 -> x0, blocking collectives: 39.6 us -> none  [the longest x1 37.1 us: on_device(): whole_norm, whole_bias = lax.psum((slope_norm[0], slope_bias[0]), 'batch')]
    unnamed x22 -> x2, local copies, waits for them, and re-layouts: 29.5 us -> 0.01 us
    unnamed x1 -> x0, blocking collectives: 19.5 us -> none
    convert_element_type x4 -> x1, other arithmetic: 14.8 us -> 0.01 us  [on_device(): halves = whole.astype(BF16)]
    slice x0 -> x4, local copies, waits for them, and re-layouts: none -> 12.8 us  [the longest x1 9.56 us: on_device(): half_down = half[1].reshape(n * rows, L).T]
  transfers between devices with their start and end apart: 4 -> 0, of which waited for: 4 -> 0; matrix products, arithmetic and copies ran while one was open for 4% -> 0% of each run, Pallas kernels for 0% -> 0%
where the time goes in v1:
time: 304 us; the launch traced here: 303 us
  Pallas kernels  260 us (86%)
  local copies, waits for them, and re-layouts  32.8 us (11%)
  other arithmetic  10.4 us (3%)
    pallas_call x1, Pallas kernels, on_device(): pl.pallas_call(functools.partial(kernel, n, m, LA), out_shape=(jax.ShapeD...  260 us
    another operation x1, local copies, waits for them, and re-layouts, on_device(): half_down = half[1].reshape(n * rows, L).T  9.63 us
    slice x1, local copies, waits for them, and re-layouts, on_device(): half_down = half[1].reshape(n * rows, L).T  9.56 us
    transpose x1, local copies, waits for them, and re-layouts, on_device(): down = slope_down[0].astype(BF16).T.reshape(Z, 2, CH, R, L)  9.5 us
    transpose x1, other arithmetic, on_device(): down = slope_down[0].astype(BF16).T.reshape(Z, 2, CH, R, L)  8.15 us

profile of v1, /device:TPU:0, one launch (start us, length us, event | category | flops | bytes accessed | tf_op | source)
XLA Modules:
  0.0 303.5 jit_solution(14111121296946785832)
XLA Ops:
  0.6 0.7 pad_maximum_fusion.1
  1.4 0.2 dynamic_update_slice.3
  1.5 0.7 pad_maximum_fusion
  2.3 0.6 reshape.44.vec_ref
  2.9 8.1 %convert_bitcast_fusion = bf16[1280,2560]{0,1:T(8,128)(2,1)} fusion(f32[1,2560,1280]{2,1,0:T(8,128)} %param.9), kind=kLoop, calls=%fused_computation | loop fusion | flops 3276800 | bytes 19660800 | tf_op jit(solution)/shard_map/transpose | solution.py:418
  11.0 9.5 %copy.16 = bf16[1280,2560]{1,0:T(8,128)(2,1)} copy(bf16[1280,2560]{0,1:T(8,128)(2,1)} %convert_bitcast_fusion) | data formatting | bytes 13107200 | tf_op jit(solution)/shard_map/transpose | solution.py:418
  20.5 259.7 %shard_map.143 = (bf16[2,4,2,10,16,2560]{5,4,3,2,1,0:T(8,128)(2,1)}, f32[20,16,2560]{2,1,0:T(8,128)}, f32[8,640]{1,0:T(8,128)}) custom-call(f32[4,2,10,16,2560]{4,3,2,1,0:T(8,128)} %bitcast.23, bf16[4,2,10,16,2560]{4,3,2,1,0:T(8,128)(2,1)} %bitcast.21, f32[10,16,2560]{2,1,0:T(8,128)} %bitcast.28, f32[10,16,2560]{2,1,0:T(8,128)} %bitcast.29, ...), custom_call_target="tpu_custom_call" | custom-call | tf_op jit(solution)/shard_map/pallas_call | solution.py:428
  280.2 0.8 multiply_subtract_fusion
  281.0 0.6 fusion.2
  281.7 0.6 slice_reduce_fusion
  282.3 9.6 %fusion = (bf16[1,4,2,10,16,2560]{5,4,3,2,1,0:T(8,128)(2,1)}, bf16[1,4,2,10,16,2560]{5,4,3,2,1,0:T(8,128)(2,1)}) fusion(bf16[2,4,2,10,16,2560]{5,4,3,2,1,0:T(8,128)(2,1)} %get-tuple-element.11), kind=kLoop, calls=%fused_computation.7 | loop fusion | bytes 26214400 | tf_op jit(solution)/shard_map/slice | solution.py:467
  291.9 0.0 copy-start
  291.9 9.6 %copy.17 = bf16[1280,2560]{0,1:T(8,128)(2,1)} copy(bf16[1280,2560]{1,0:T(8,128)(2,1)} %bitcast.22) | data formatting | bytes 13107200 | tf_op jit(solution)/shard_map/reshape;squeeze | solution.py:467
  301.5 0.0 copy-done
  301.5 2.0 fusion.1
  (3 shorter events, 0.0 us)
Async XLA Ops:
  291.9 9.6 %copy-start = (f32[20,16,2560]{2,1,0:T(8,128)S(1)}, f32[20,16,2560]{2,1,0:T(8,128)}, u32[]{:S(2)}) copy-start(f32[20,16,2560]{2,1,0:T(8,128)} %get-tuple-element.13) | copy-start | bytes 9830404

commit v2 on v1

--- a/solution.py
+++ b/solution.py
@@ -9,8 +9,9 @@
 
 learn_rate = 0.4
 MESH = pl.DeviceIdType.MESH
-R = 16
+R = 8
 LANE = 128
+SPLIT = 0.6
 F32, BF16 = jnp.float32, jnp.bfloat16
 
 
@@ -23,10 +24,12 @@
     pup_ref,
     pdown_ref,
     vec_ref,
-    half_ref,
+    half_up_ref,
+    half_down_ref,
     next_ref,
     sums_ref,
     stage,
+    turn,
     XA,
     XB,
     RYA,
@@ -64,19 +67,40 @@
     def load_up(c):
         return pltpu.make_async_copy(up_ref.at[:, :, c], stage.at[c % 2], up_sem.at[c % 2])
 
-    def load_down(c):
-        k = c - CH
-        return [
-            pltpu.make_async_copy(
-                down_ref.at[:, 0, k, :, pl.ds(0, LA)], XA.at[c, 0], down_sem.at[0, k]
-            ),
-            pltpu.make_async_copy(
-                down_ref.at[:, 1, k, :, pl.ds(0, LA)], XA.at[c, 1], down_sem.at[1, k]
-            ),
-            pltpu.make_async_copy(
-                down_ref.at[:, :, k, :, pl.ds(LA, L - LA)], XB.at[c], down_sem.at[2, k]
-            ),
-        ]
+    blocks = L // LANE
+    share = -(-blocks // CH)
+
+    def load_down(b):
+        return pltpu.make_async_copy(
+            down_ref.at[pl.ds(b * LANE, LANE)], turn.at[b % 2], down_sem.at[b % 2]
+        )
+
+    def turn_block(b):
+        def pieces(store):
+            for j in range(n * CH * R // LANE):
+                tile = turn[b % 2, :, j * LANE : (j + 1) * LANE].T
+                for i in range(LANE // R):
+                    piece = j * (LANE // R) + i
+                    d, k = piece // CH, piece % CH
+                    store(d // 2, d % 2, CH + k, tile[i * R : (i + 1) * R].astype(BF16))
+
+        @pl.when(b * LANE < LA)
+        def _():
+            at = pl.ds(pl.multiple_of(b * LANE, LANE), LANE)
+
+            def store(d, v, c, x):
+                XA[c, v, d, :, at] = x
+
+            pieces(store)
+
+        @pl.when(b * LANE >= LA)
+        def _():
+            at = pl.ds(pl.multiple_of(b * LANE - LA, LANE), LANE)
+
+            def store(d, v, c, x):
+                XB[c, d, v, :, at] = x
+
+            pieces(store)
 
     def load_params():
         return [
@@ -88,10 +112,7 @@
     for d in load_params():
         d.start()
 
-    @pl.loop(CH, C)
-    def _(c):
-        for d in load_down(c):
-            d.start()
+    load_down(0).start()
 
     barrier = pltpu.get_barrier_semaphore()
     for o in range(1, n):
@@ -247,20 +268,28 @@
                 if k > 0:
                     gather_left(first, c, k).start()
 
-    def outs(c):
-        w = c // CH
-        k = c % CH
-        return [
-            pltpu.make_async_copy(
-                GA.at[c, 0], half_ref.at[w, :, 0, k, :, pl.ds(0, LA)], out_sem.at[0, c]
-            ),
-            pltpu.make_async_copy(
-                GA.at[c, 1], half_ref.at[w, :, 1, k, :, pl.ds(0, LA)], out_sem.at[1, c]
-            ),
-            pltpu.make_async_copy(
-                GB.at[c], half_ref.at[w, :, :, k, :, pl.ds(LA, L - LA)], out_sem.at[2, c]
-            ),
-        ]
+    def outs(c, act):
+        def each(half_ref, k):
+            for d in (
+                pltpu.make_async_copy(
+                    GA.at[c, 0], half_ref.at[:, 0, k, :, pl.ds(0, LA)], out_sem.at[0, c]
+                ),
+                pltpu.make_async_copy(
+                    GA.at[c, 1], half_ref.at[:, 1, k, :, pl.ds(0, LA)], out_sem.at[1, c]
+                ),
+                pltpu.make_async_copy(
+                    GB.at[c], half_ref.at[:, :, k, :, pl.ds(LA, L - LA)], out_sem.at[2, c]
+                ),
+            ):
+                act(d)
+
+        @pl.when(c < CH)
+        def _():
+            each(half_up_ref, c)
+
+        @pl.when(c >= CH)
+        def _():
+            each(half_down_ref, c - CH)
 
     def next_out(c):
         return pltpu.make_async_copy(NX.at[c], next_ref.at[c], out_sem.at[3, c])
@@ -289,14 +318,21 @@
                     XA[t, v, d] = stage[t % 2, d, v, :, :LA].astype(BF16)
                     XB[t, d, v] = stage[t % 2, d, v, :, LA:].astype(BF16)
 
-        @pl.when((t >= CH) & (t < C))
-        def _():
-            for d in load_down(t):
-                d.wait()
-
         @pl.when(t < C)
         def _():
             ya(t).start()
+
+        for i in range(share):
+            b = t * share + i
+
+            @pl.when(b + 1 < blocks)
+            def _():
+                load_down(b + 1).start()
+
+            @pl.when(b < blocks)
+            def _():
+                load_down(b).wait()
+                turn_block(b)
 
         reduce_step(False, t)
         s = t - 1
@@ -370,8 +406,7 @@
         @when_chunk(e)
         def _():
             gya_in(e).wait_recv()
-            for d in outs(e):
-                d.start()
+            outs(e, lambda d: d.start())
 
     total = vec_ref[...]
     for o in range(1, n):
@@ -381,8 +416,7 @@
 
     @pl.loop(0, C)
     def _(c):
-        for d in outs(c):
-            d.wait()
+        outs(c, lambda d: d.wait())
         next_out(c).wait()
         for d in (ya(c), yb(c), gya(c), gyb(c)):
             d.wait_send()
@@ -410,12 +444,12 @@
     rows, L = param_up.shape
     CH = rows // R
     C = 2 * CH
-    LA = max(1, round(0.6 * L / LANE)) * LANE
+    LA = max(1, round(SPLIT * L / LANE)) * LANE
     LB = L - LA
     width = slope_norm.shape[1]
     place = lax.axis_index("batch")
     up = slope_up[0].reshape(Z, 2, CH, R, L)
-    down = slope_down[0].astype(BF16).T.reshape(Z, 2, CH, R, L)
+    down = slope_down[0]
     pup = param_up.reshape(CH, R, L)
     pdown = param_down.T.reshape(CH, R, L)
     mine = lax.dynamic_update_slice(
@@ -425,17 +459,19 @@
     kinds = 12
     hbm = pl.BlockSpec(memory_space=pl.ANY)
     vmem = pl.BlockSpec(memory_space=pltpu.VMEM)
-    half, new, sums = pl.pallas_call(
+    half_up, half_down, new, sums = pl.pallas_call(
         functools.partial(kernel, n, m, LA),
         out_shape=(
-            jax.ShapeDtypeStruct((2, Z, 2, CH, R, L), BF16),
+            jax.ShapeDtypeStruct((Z, 2, CH, R, L), BF16),
+            jax.ShapeDtypeStruct((Z, 2, CH, R, L), BF16),
             jax.ShapeDtypeStruct((C, R, L), F32),
             jax.ShapeDtypeStruct(vec.shape, F32),
         ),
         in_specs=[hbm, hbm, hbm, hbm, vmem],
-        out_specs=(hbm, hbm, vmem),
+        out_specs=(hbm, hbm, hbm, vmem),
         scratch_shapes=[
             pltpu.VMEM((2, Z, 2, R, L), F32),
+            pltpu.VMEM((2, LANE, n * rows), F32),
             pltpu.VMEM((C, 2, Z, R, LA), BF16),
             pltpu.VMEM((C, Z, 2, R, LB), BF16),
             pltpu.VMEM((C, Z, R, LA), BF16),
@@ -449,7 +485,7 @@
             pltpu.VMEM((C, Z, 2, R, LB), BF16),
             pltpu.VMEM((n - 1,) + vec.shape, F32),
             pltpu.SemaphoreType.DMA((2,)),
-            pltpu.SemaphoreType.DMA((3, CH)),
+            pltpu.SemaphoreType.DMA((2,)),
             pltpu.SemaphoreType.DMA((2,)),
             pltpu.SemaphoreType.DMA((4, C)),
             pltpu.SemaphoreType.DMA((kinds, C)),
@@ -463,8 +499,8 @@
             collective_id=0, has_side_effects=True, vmem_limit_bytes=67043328
         ),
     )(up, down, pup, pdown, vec)
-    half_up = half[0].reshape(n * rows, L)
-    half_down = half[1].reshape(n * rows, L).T
+    half_up = half_up.reshape(n * rows, L)
+    half_down = half_down.reshape(n * rows, L).T
     next_up = new[:CH].reshape(rows, L)
     next_down = new[CH:].reshape(rows, L).T
     sums = sums.reshape(4, width)

time: 304 us -> 271 us (0.89)
  Pallas kernels: 260 us -> 246 us
  local copies, waits for them, and re-layouts: 32.8 us -> 21.5 us
  other arithmetic: 10.4 us -> 2.25 us
    pallas_call x1, Pallas kernels: 260 us -> 246 us  [on_device(): pl.pallas_call(functools.partial(kernel, n, m, LA), out_shape=(jax.ShapeD...]
    slice x2 -> x0, local copies, waits for them, and re-layouts: 11.5 us -> none  [the longest x1 9.56 us: on_device(): half_down = half[1].reshape(n * rows, L).T]
    another operation x1 -> x0, local copies, waits for them, and re-layouts: 9.63 us -> none  [on_device(): half_down = half[1].reshape(n * rows, L).T]
    reshape x0 -> x1, local copies, waits for them, and re-layouts: none -> 9.48 us  [on_device(): half_down = half_down.reshape(n * rows, L).T]
    transpose x1 -> x0, other arithmetic: 8.15 us -> none  [on_device(): down = slope_down[0].astype(BF16).T.reshape(Z, 2, CH, R, L)]
    unnamed x2 -> x1, local copies, waits for them, and re-layouts: 0.01 us -> 6.07 us
    transpose x1, local copies, waits for them, and re-layouts: 9.5 us -> 3.85 us  [on_device(): next_down = new[CH:].reshape(rows, L).T]
where the time goes in v2:
time: 271 us; the launch traced here: 270 us
  Pallas kernels  246 us (91%)
  local copies, waits for them, and re-layouts  21.5 us (8%)
    pallas_call x1, Pallas kernels, on_device(): pl.pallas_call(functools.partial(kernel, n, m, LA), out_shape=(jax.ShapeD...  246 us
    reshape x1, local copies, waits for them, and re-layouts, on_device(): half_down = half_down.reshape(n * rows, L).T  9.48 us
    unnamed x1, local copies, waits for them, and re-layouts  6.07 us

profile of v2, /device:TPU:0, one launch (start us, length us, event | category | flops | bytes accessed | tf_op | source)
XLA Modules:
  0.0 270.1 jit_solution(4732298112391045332)
XLA Ops:
  0.6 0.7 pad_maximum_fusion.1
  1.4 0.2 dynamic_update_slice.3
  1.5 0.7 pad_maximum_fusion
  2.3 0.6 reshape.45.vec_ref
  2.9 245.7 %shard_map.143 = (bf16[4,2,20,8,2560]{4,3,2,1,0:T(8,128)(2,1)}, bf16[4,2,20,8,2560]{4,3,2,1,0:T(8,128)(2,1)}, f32[40,8,2560]{2,1,0:T(8,128)}, f32[8,640]{1,0:T(8,128)}) custom-call(f32[4,2,20,8,2560]{4,3,2,1,0:T(8,128)} %bitcast.19, f32[2560,1280]{1,0:T(8,128)} %bitcast.20, f32[20,8,2560]{2,1,0:T(8,128)} %bitcast.24, f32[20,8,2560]{2,1,0:T(8,128)} %bitcast.25, ...), custom_call_target="tpu_custom_call" | custom-call | tf_op jit(solution)/shard_map/pallas_call | solution.py:462
  248.6 0.8 multiply_subtract_fusion
  249.5 0.6 fusion
  250.1 0.6 slice_reduce_fusion
  250.7 3.8 %slice_bitcast_fusion = (f32[2560,160]{0,1:T(8,128)}, f32[160,2560]{1,0:T(8,128)}) fusion(f32[40,8,2560]{2,1,0:T(8,128)} %get-tuple-element.15), kind=kLoop, calls=%fused_computation | loop fusion | bytes 6553600 | tf_op jit(solution)/shard_map/transpose | solution.py:505
  254.6 9.5 %copy.16 = bf16[1280,2560]{0,1:T(8,128)(2,1)} copy(bf16[1280,2560]{1,0:T(8,128)(2,1)} %bitcast.22) | data formatting | bytes 13107200 | tf_op jit(solution)/shard_map/reshape | solution.py:503
  264.1 6.1 %copy.19 = bf16[1280,2560]{1,0:T(8,128)(2,1)} copy(bf16[1280,2560]{1,0:T(8,128)(2,1)} %bitcast.21) | data formatting | bytes 13107200
  (3 shorter events, 0.0 us)

commit v3 on v2

--- a/solution.py
+++ b/solution.py
@@ -26,7 +26,8 @@
     vec_ref,
     half_up_ref,
     half_down_ref,
-    next_ref,
+    next_up_ref,
+    next_down_ref,
     sums_ref,
     stage,
     turn,
@@ -291,8 +292,14 @@
         def _():
             each(half_down_ref, c - CH)
 
-    def next_out(c):
-        return pltpu.make_async_copy(NX.at[c], next_ref.at[c], out_sem.at[3, c])
+    def next_out(c, act):
+        @pl.when(c < CH)
+        def _():
+            act(pltpu.make_async_copy(NX.at[c], next_up_ref.at[c], out_sem.at[3, c]))
+
+        @pl.when(c >= CH)
+        def _():
+            act(pltpu.make_async_copy(NX.at[c], next_down_ref.at[c - CH], out_sem.at[3, c]))
 
     def lanes(x):
         s = x[:, :LANE] * x[:, :LANE]
@@ -304,7 +311,7 @@
     def when_chunk(c):
         return pl.when((c >= 0) & (c < C))
 
-    @pl.loop(0, C + 2 * Z + 2)
+    @pl.loop(0, C + 2 * Z)
     def _(t):
         @pl.when(t + 1 < CH)
         def _():
@@ -321,18 +328,6 @@
         @pl.when(t < C)
         def _():
             ya(t).start()
-
-        for i in range(share):
-            b = t * share + i
-
-            @pl.when(b + 1 < blocks)
-            def _():
-                load_down(b + 1).start()
-
-            @pl.when(b < blocks)
-            def _():
-                load_down(b).wait()
-                turn_block(b)
 
         reduce_step(False, t)
         s = t - 1
@@ -367,7 +362,19 @@
             for o in range(1, m):
                 sq_copy(f, o).start()
 
-        u = t - Z - 1
+        u = t - Z
+
+        @when_chunk(u - 1)
+        def _():
+            gyb_in(u - 1).wait_recv()
+
+        gather_step(False, u - 1)
+        e = u - Z
+
+        @when_chunk(e)
+        def _():
+            gya_in(e).wait_recv()
+            outs(e, lambda d: d.start())
 
         @when_chunk(u)
         def _():
@@ -387,26 +394,25 @@
             GA[u, y, z] = half[:, :LA]
             GB[u, z, y] = half[:, LA:]
             gyb(u).start()
-            next_out(u).start()
+            next_out(u, lambda d: d.start())
 
         gather_step(True, u)
 
-        @when_chunk(u - 1)
-        def _():
-            gyb_in(u - 1).wait_recv()
-
-        gather_step(False, u - 1)
-
         @when_chunk(u - (Z - 1))
         def _():
             gya(u - (Z - 1)).start()
 
-        e = u - Z
-
-        @when_chunk(e)
-        def _():
-            gya_in(e).wait_recv()
-            outs(e, lambda d: d.start())
+        for i in range(share):
+            b = t * share + i
+
+            @pl.when(b + 1 < blocks)
+            def _():
+                load_down(b + 1).start()
+
+            @pl.when(b < blocks)
+            def _():
+                load_down(b).wait()
+                turn_block(b)
 
     total = vec_ref[...]
     for o in range(1, n):
@@ -417,7 +423,7 @@
     @pl.loop(0, C)
     def _(c):
         outs(c, lambda d: d.wait())
-        next_out(c).wait()
+        next_out(c, lambda d: d.wait())
         for d in (ya(c), yb(c), gya(c), gyb(c)):
             d.wait_send()
         for o in range(1, m):
@@ -459,16 +465,17 @@
     kinds = 12
     hbm = pl.BlockSpec(memory_space=pl.ANY)
     vmem = pl.BlockSpec(memory_space=pltpu.VMEM)
-    half_up, half_down, new, sums = pl.pallas_call(
+    half_up, half_down, new_up, new_down, sums = pl.pallas_call(
         functools.partial(kernel, n, m, LA),
         out_shape=(
             jax.ShapeDtypeStruct((Z, 2, CH, R, L), BF16),
             jax.ShapeDtypeStruct((Z, 2, CH, R, L), BF16),
-            jax.ShapeDtypeStruct((C, R, L), F32),
+            jax.ShapeDtypeStruct((CH, R, L), F32),
+            jax.ShapeDtypeStruct((CH, R, L), F32),
             jax.ShapeDtypeStruct(vec.shape, F32),
         ),
         in_specs=[hbm, hbm, hbm, hbm, vmem],
-        out_specs=(hbm, hbm, hbm, vmem),
+        out_specs=(hbm, hbm, hbm, hbm, vmem),
         scratch_shapes=[
             pltpu.VMEM((2, Z, 2, R, L), F32),
             pltpu.VMEM((2, LANE, n * rows), F32),
@@ -501,8 +508,8 @@
     )(up, down, pup, pdown, vec)
     half_up = half_up.reshape(n * rows, L)
     half_down = half_down.reshape(n * rows, L).T
-    next_up = new[:CH].reshape(rows, L)
-    next_down = new[CH:].reshape(rows, L).T
+    next_up = new_up.reshape(rows, L)
+    next_down = new_down.reshape(rows, L).T
     sums = sums.reshape(4, width)
     whole = sums[2:] - learn_rate * (sums[:2] * n ** (-0.5))
     own = lax.dynamic_slice_in_dim(whole, place * rows, rows, axis=1)

time: 271 us -> 267 us (0.985)
    transpose x1 -> x0, local copies, waits for them, and re-layouts: 3.85 us -> none  [on_device(): next_down = new[CH:].reshape(rows, L).T]
    unnamed x1 -> x7, local copies, waits for them, and re-layouts: 6.07 us -> 8.56 us
where the time goes in v3:
time: 267 us
  Pallas kernels  244 us (91%)
  local copies, waits for them, and re-layouts  20.1 us (8%)
    pallas_call x1, Pallas kernels, on_device(): pl.pallas_call(functools.partial(kernel, n, m, LA), out_shape=(jax.ShapeD...  244 us
    reshape x1, local copies, waits for them, and re-layouts, on_device(): half_down = half_down.reshape(n * rows, L).T  9.48 us
    unnamed x7, local copies, waits for them, and re-layouts  8.56 us

profile of v3, /device:TPU:0, one launch (start us, length us, event | category | flops | bytes accessed | tf_op | source)
XLA Modules:
  0.0 266.8 jit_solution(11690720012033683737)
XLA Ops:
  0.6 0.7 pad_maximum_fusion.1
  1.4 0.2 dynamic_update_slice.3
  1.5 0.7 pad_maximum_fusion
  2.3 0.6 reshape.45.vec_ref
  2.9 243.8 %shard_map.143 = (bf16[4,2,20,8,2560]{4,3,2,1,0:T(8,128)(2,1)}, bf16[4,2,20,8,2560]{4,3,2,1,0:T(8,128)(2,1)}, f32[20,8,2560]{2,1,0:T(8,128)}, f32[20,8,2560]{2,1,0:T(8,128)}, f32[8,640]{1,0:T(8,128)}) custom-call(f32[4,2,20,8,2560]{4,3,2,1,0:T(8,128)} %bitcast.17, f32[2560,1280]{1,0:T(8,128)} %bitcast.18, f32[20,8,2560]{2,1,0:T(8,128)} %bitcast.24, ...), custom_call_target="tpu_custom_call" | custom-call | tf_op jit(solution)/shard_map/pallas_call | solution.py:468
  246.7 0.8 multiply_subtract_fusion
  247.5 0.6 fusion
  248.1 0.6 slice_reduce_fusion
  248.8 9.5 %copy.16 = bf16[1280,2560]{0,1:T(8,128)(2,1)} copy(bf16[1280,2560]{1,0:T(8,128)(2,1)} %bitcast.20) | data formatting | bytes 13107200 | tf_op jit(solution)/shard_map/reshape | solution.py:510
  258.2 0.0 copy-start.1
  258.2 0.0 copy-start
  258.2 6.2 %copy.21 = bf16[1280,2560]{1,0:T(8,128)(2,1)} copy(bf16[1280,2560]{1,0:T(8,128)(2,1)} %bitcast.19) | data formatting | bytes 13107200
  264.5 0.0 copy-done.1
  264.5 1.2 copy.22
  265.6 0.0 copy-done
  265.6 1.2 copy.23
  (3 shorter events, 0.0 us)
Async XLA Ops:
  258.2 6.2 %copy-start.1 = (f32[20,8,2560]{2,1,0:T(8,128)S(1)}, f32[20,8,2560]{2,1,0:T(8,128)}, u32[]{:S(2)}) copy-start(f32[20,8,2560]{2,1,0:T(8,128)} %get-tuple-element.16) | copy-start | bytes 4915204
  258.2 7.4 %copy-start = (f32[20,8,2560]{2,1,0:T(8,128)S(1)}, f32[20,8,2560]{2,1,0:T(8,128)}, u32[]{:S(2)}) copy-start(f32[20,8,2560]{2,1,0:T(8,128)} %get-tuple-element.17) | copy-start | bytes 4915204
